TPU v7x, 256 devices: a 4x2x16 block of a 4x16x16 slice. The times are simulated.
256 devices in a mesh: groups: 2 (over y), seq: 16 (over z), batch: 4 (over x), head: 2 (over core).
Axes of the slice: x: 4, y: 2, z: 16, core: 2. Of those that a mesh axis runs over, the one named last changes fastest.
The devices are a block of a 4x16x16 slice.
Arguments:
- hidden_in: bfloat16 [128, 4096], P(('groups', 'batch'), 'seq'), parts along dimension 0, may hold values from -400 to 400
- norm_gain_vector: bfloat16 [4096], P('seq'), may hold values from 0.099609375 to 1.8984375
- w_query: bfloat16 [4096, 4096], P('seq', 'head'), may hold values from -0.09375 to 0.09375
- key_cache_rows: bfloat16 [128, 16384, 128], P(('groups', 'batch'), 'seq'), parts along dimension 0, may hold values from -360 to 360
- value_cache_rows: bfloat16 [128, 16384, 128], P(('groups', 'batch'), 'seq'), parts along dimension 0, may hold values from -6 to 6
- k_new: bfloat16 [128, 128], P(('groups', 'batch')), parts along dimension 0, may hold values from -360 to 360
- v_new: bfloat16 [128, 128], P(('groups', 'batch')), parts along dimension 0, may hold values from -6 to 6
- lengths: int32 [128], P(('groups', 'batch')), parts along dimension 0, may hold values from 1 to 16384, as said below
- w_out: bfloat16 [4096, 4096], P('head', 'seq'), may hold values from -0.09375 to 0.09375
Outputs:
- layer_out: float32 [128, 4096], P(('groups', 'batch'), ('seq', 'head')), parts along dimension 0
There are 2 independent parts, one for each index of `groups`. A program takes and returns all parts, laid end to end along the dimension named above; an argument that names none is the same for every part. Nothing has to cross between parts.
Inputs may be any that keep to these rules, and one draw needn't show every extreme that they name: `lengths`: every sequence has at least one cached position; some sequence of each draw uses all 16384.
All inputs are finite; a program needn't handle non-finite values.
Results may differ from a plain program's by a relative error of at most 0.008.
Values sent between devices are 32-bit elements; how exact they have to be, the bound alone decides.
No kernel may reach another device: no remote copies, remote signals or barrier semaphores. Data moves between devices by JAX's collectives and lax.ppermute only.
A program may use at most 64 MiB of HBM per device.

v0:
```python
import jax
import jax.numpy as jnp
from jax import lax
from jax.sharding import PartitionSpec as P

D = 4096
HD = 128


def sent_to_all(array, axis):
    copies = jnp.broadcast_to(array, (lax.axis_size(axis), *array.shape))
    return lax.all_to_all(copies, axis, split_axis=0, concat_axis=0, tiled=True)


def of_everyone(array, axis):
    everything = sent_to_all(array, axis)
    return jnp.sum(everything, axis=0)


def padded_to(lines, length):
    spare = -lines.shape[0] % length
    if not spare:
        return lines
    return jnp.concatenate([lines, jnp.zeros((spare, *lines.shape[1:]), lines.dtype)])


def in_order(blocks, dim):
    shape = list(blocks.shape[1:])
    shape[dim] *= blocks.shape[0]
    return jnp.moveaxis(blocks, 0, dim).reshape(shape)


def collect(array, axis, dim):
    blocks = sent_to_all(array, axis)
    return in_order(blocks, dim)


def cut_along(array, dim, length):
    shape = array.shape
    blocks = array.reshape(*shape[:dim], length, shape[dim] // length, *shape[dim + 1 :])
    return jnp.moveaxis(blocks, dim, 0)


def sent_and_summed(array, axis, dim):
    length = lax.axis_size(axis)
    blocks = lax.all_to_all(cut_along(array, dim, length), axis, 0, 0, tiled=True)
    return jnp.sum(blocks, axis=0)


def total_of(array, axes):
    lines = array.reshape(-1, array.shape[-1])
    padded = padded_to(lines, lax.axis_size(axes))
    whole = collect(sent_and_summed(padded, axes, 0), axes, 0)
    return lax.slice_in_dim(whole, 0, len(lines)).reshape(array.shape)


def taken_together(array, axis):
    return sent_to_all(array, axis).max(axis=0)


def nested_sum(array, axes):
    padded = padded_to(array, lax.axis_size(axes))
    whole = collect(sent_and_summed(padded, axes, 0), axes, 0)
    return lax.slice_in_dim(whole, 0, len(array)).reshape(array.shape)


def together(arrays, axis):
    ravelled, at, gathered = (jnp.concatenate([a.reshape(-1) for a in arrays]), 0, [])
    total = nested_sum(ravelled, axis)
    for a in arrays:
        gathered.append(total[at : at + a.size].reshape(a.shape))
        at += a.size
    return tuple(gathered)


def shards(
    hidden_in,
    norm_gain_vector,
    w_query,
    key_cache_rows,
    value_cache_rows,
    k_new,
    v_new,
    lengths,
    w_out,
):
    inputs = hidden_in.astype(jnp.float32)
    squares = of_everyone(jnp.sum(inputs * inputs, axis=-1), "seq")
    inv_rms = lax.rsqrt(squares / D + 1e-05)
    normed = (inputs * inv_rms[:, None] * norm_gain_vector.astype(jnp.float32)[None, :]).astype(
        jnp.bfloat16
    )
    partial_query = jnp.dot(normed, w_query, preferred_element_type=jnp.float32)
    inverse_root_norm = 1.0 / HD**0.5
    query_vectors = (total_of(partial_query, "seq") * inverse_root_norm).astype(jnp.bfloat16)
    seq_rows = query_vectors.shape[0]
    query_vectors = query_vectors.reshape(seq_rows, query_vectors.shape[1] // HD, HD)
    block_len = key_cache_rows.shape[1]
    scores = jnp.einsum(
        "irm,iam->ira", query_vectors, key_cache_rows, preferred_element_type=jnp.float32
    )
    own = jnp.einsum("bhd,bd->bh", query_vectors, k_new, preferred_element_type=jnp.float32)
    positions = lax.axis_index("seq") * block_len + lax.iota(jnp.int32, block_len)
    live_mask = (positions[None, :] < lengths[:, None])[:, None, :]
    local_top = jnp.maximum(jnp.max(jnp.where(live_mask, scores, -jnp.inf), axis=-1), own)
    softmax_weights = jnp.where(live_mask, jnp.exp(scores - local_top[..., None]), jnp.float32(0.0))
    local_total = jnp.sum(softmax_weights, axis=-1)
    local_partial_sum = jnp.einsum(
        "ajq,aqe->aje",
        softmax_weights.astype(jnp.bfloat16),
        value_cache_rows,
        preferred_element_type=jnp.float32,
    )
    top = taken_together(local_top, "seq")
    factor = jnp.exp(local_top - top)
    totals, summed = together((local_total * factor, local_partial_sum * factor[..., None]), "seq")
    fresh = jnp.exp(own - top)
    totals = totals + fresh
    result = (summed + fresh[..., None] * v_new.astype(jnp.float32)[:, None, :]) / totals[..., None]
    attended = result.astype(jnp.bfloat16).reshape(seq_rows, -1)
    partial_out = jnp.dot(attended, w_out, preferred_element_type=jnp.float32)
    return sent_and_summed(partial_out, "head", 1)


def solution(mesh):
    placed = (
        P(("groups", "batch"), "seq"),
        P("seq"),
        P("seq", "head"),
        P(("groups", "batch"), "seq", None),
        P(("groups", "batch"), "seq", None),
        P(("groups", "batch"), None),
        P(("groups", "batch"), None),
        P(("groups", "batch")),
        P("head", "seq"),
    )
    return jax.shard_map(
        shards,
        mesh=mesh,
        in_specs=placed,
        out_specs=P(("groups", "batch"), ("seq", "head")),
        check_vma=False,
    )
```

profile of v0, /device:TPU:33, one launch (start us, length us, event | category | flops | bytes accessed | tf_op | source)
XLA Modules:
  0.0 140.8 jit_solution(7930594931385334145)
XLA Ops:
  0.0 0.9 fusion.6
  0.9 0.6 broadcast_in_dim.45
  1.5 24.5 %all-to-all-start = ((f32[16,1,16]{2,1,0:T(1,128)}), f32[16,1,16]{2,1,0:T(1,128)S(1)}, u32[]{:S(2)}, u32[]{:S(2)}) async-start(f32[16,1,16]{2,1,0:T(1,128)} %broadcast_in_dim.45), calls=%async_computation | async-start | bytes 16384 | tf_op jit(solution)/shard_map/all_to_all | solution.py:12
  26.0 0.7 convert_element_type.36
  26.7 10.4 %all-to-all-done = f32[16,1,16]{2,1,0:T(1,128)S(1)} async-done(((f32[16,1,16]{2,1,0:T(1,128)}), f32[16,1,16]{2,1,0:T(1,128)S(1)}, u32[]{:S(2)}, u32[]{:S(2)}) %all-to-all-start) | async-done | bytes 1056 | tf_op jit(solution)/shard_map/all_to_all | solution.py:12
  37.1 1.0 convolution_bitcast_fusion
  38.3 14.6 %all_to_all.41 = f32[16,1,2048]{2,1,0:T(1,128)S(1)} all-to-all(f32[16,1,2048]{2,1,0:T(1,128)S(1)} %copy.19), channel_id=1, replica_groups=mesh['groups'=2,'seq'=16,'batch'=4,'head'=2] {'seq'}, dimensions={0} | all-to-all | bytes 262144 | tf_op jit(solution)/shard_map/all_to_all | solution.py:46
  52.9 0.7 broadcast_in_dim.46
  53.7 5.6 %all-to-all-start.2 = ((f32[16,1,2048]{2,1,0:T(1,128)}), f32[16,1,2048]{2,1,0:T(1,128)S(1)}, u32[]{:S(2)}, u32[]{:S(2)}) async-start(f32[16,1,2048]{2,1,0:T(1,128)} %broadcast_in_dim.46), calls=%async_computation.2 | async-start | bytes 262144 | tf_op jit(solution)/shard_map/all_to_all | solution.py:12
  59.2 0.7 broadcast_compare_fusion
  60.0 11.0 %all-to-all-done.2 = f32[16,1,2048]{2,1,0:T(1,128)S(1)} async-done(((f32[16,1,2048]{2,1,0:T(1,128)}), f32[16,1,2048]{2,1,0:T(1,128)S(1)}, u32[]{:S(2)}, u32[]{:S(2)}) %all-to-all-start.2) | async-done | bytes 131104 | tf_op jit(solution)/shard_map/all_to_all | solution.py:12
  71.0 0.4 convert_reduce_fusion
  71.4 0.8 fusion.10
  72.2 3.5 %select_reduce_fusion = (f32[16,16]{1,0:T(8,128)S(1)}, f32[16,16,1024]{2,1,0:T(8,128)S(1)}) fusion(pred[16,1024]{1,0:T(8,128)(4,1)S(1)} %broadcast_compare_fusion, bf16[16,16,128]{2,1,0:T(8,128)(2,1)S(1)} %bitcast.27, bf16[16,1024,128]{2,1,0:T(8,128)(2,1)} %param.12), kind=kOutput, calls=%fused_computation.4 | convolution fusion | flops 67632896 | bytes 5325824 | tf_op jit(solution)/shard_map/irm,iam->ira/dot_general | solution.py:99
  75.7 0.7 reshape.117
  76.5 5.5 %all-to-all-start.3 = ((f32[16,1,256]{2,1,0:T(1,128)}), f32[16,1,256]{2,1,0:T(1,128)S(1)}, u32[]{:S(2)}, u32[]{:S(2)}) async-start(f32[16,1,256]{2,1,0:T(1,128)} %reshape.117), calls=%async_computation.3 | async-start | bytes 32768 | tf_op jit(solution)/shard_map/all_to_all | solution.py:12
  81.9 0.3 fusion.1
  82.3 10.8 %all-to-all-done.3 = f32[16,1,256]{2,1,0:T(1,128)S(1)} async-done(((f32[16,1,256]{2,1,0:T(1,128)}), f32[16,1,256]{2,1,0:T(1,128)S(1)}, u32[]{:S(2)}, u32[]{:S(2)}) %all-to-all-start.3) | async-done | bytes 16416 | tf_op jit(solution)/shard_map/all_to_all | solution.py:12
  93.1 0.5 broadcast.70
  93.6 0.7 reduce.7
  94.5 2.9 %convolution_multiply_fusion = f32[16,16,128]{2,1,0:T(8,128)S(1)} fusion(bf16[16,1024,128]{2,1,0:T(8,128)(2,1)} %param.13, f32[16,16,1024]{2,1,0:T(8,128)S(1)} %get-tuple-element.10, f32[16,16]{1,0:T(8,128)S(1)} %max.3, pred[16,1024]{1,0:T(8,128)(4,1)S(1)} %broadcast_compare_fusion, f32[16,16]{1,0:T(8,128)S(1)} %get-tuple-element.8), kind=kOutput, calls=%fused_computation.1 | convolution fusion | flops 67928064 | bytes 5392384 | tf_op jit(solution)/shard_map/ajq,aqe->aje/dot_general | solution.py:108
  97.5 0.2 all_to_all.30
  97.7 14.6 %all_to_all.42 = f32[16,1,2064]{2,1,0:T(1,128)S(1)} all-to-all(f32[16,1,2064]{2,1,0:T(1,128)S(1)} %all_to_all.30), channel_id=1, replica_groups=mesh['groups'=2,'seq'=16,'batch'=4,'head'=2] {'seq'}, dimensions={0} | all-to-all | bytes 264192 | tf_op jit(solution)/shard_map/all_to_all | solution.py:46
  112.5 0.7 broadcast_in_dim.50
  113.2 4.4 %all-to-all-start.5 = ((f32[16,1,2064]{2,1,0:T(1,128)}), f32[16,1,2064]{2,1,0:T(1,128)S(1)}, u32[]{:S(2)}, u32[]{:S(2)}) async-start(f32[16,1,2064]{2,1,0:T(1,128)} %broadcast_in_dim.50), calls=%async_computation.5 | async-start | bytes 278528 | tf_op jit(solution)/shard_map/all_to_all | solution.py:12
  117.7 0.6 copy.24
  118.3 11.2 %all-to-all-done.5 = f32[16,1,2064]{2,1,0:T(1,128)S(1)} async-done(((f32[16,1,2064]{2,1,0:T(1,128)}), f32[16,1,2064]{2,1,0:T(1,128)S(1)}, u32[]{:S(2)}, u32[]{:S(2)}) %all-to-all-start.5) | async-done | bytes 132128 | tf_op jit(solution)/shard_map/all_to_all | solution.py:12
  129.5 0.3 reduce.4
  129.8 0.3 slice.10
  130.4 0.4 convolution_bitcast_fusion.1
  130.8 9.4 %all_to_all.43 = f32[2,16,128]{2,1,0:T(8,128)S(1)} all-to-all(f32[2,16,128]{2,1,0:T(8,128)S(1)} %convolution_bitcast_fusion.1), channel_id=1, replica_groups=mesh['groups'=2,'seq'=16,'batch'=4,'head'=2] {'head'}, dimensions={0} | all-to-all | bytes 32768 | tf_op jit(solution)/shard_map/all_to_all | solution.py:46
  140.2 0.6 reduce_sum.59
  (26 shorter events, 0.9 us)
Async XLA Ops:
  0.0 37.1 %copy-start = (bf16[256,2048]{1,0:T(8,128)(2,1)S(1)}, bf16[256,2048]{1,0:T(8,128)(2,1)}, u32[]{:S(2)}) copy-start(bf16[256,2048]{1,0:T(8,128)(2,1)} %param.11) | copy-start | bytes 3145732
  1.5 35.6 %all-to-all-start = ((f32[16,1,16]{2,1,0:T(1,128)}), f32[16,1,16]{2,1,0:T(1,128)S(1)}, u32[]{:S(2)}, u32[]{:S(2)}) async-start(f32[16,1,16]{2,1,0:T(1,128)} %broadcast_in_dim.45), calls=%async_computation | async-start | bytes 16384 | tf_op jit(solution)/shard_map/all_to_all | solution.py:12
  53.7 17.3 %all-to-all-start.2 = ((f32[16,1,2048]{2,1,0:T(1,128)}), f32[16,1,2048]{2,1,0:T(1,128)S(1)}, u32[]{:S(2)}, u32[]{:S(2)}) async-start(f32[16,1,2048]{2,1,0:T(1,128)} %broadcast_in_dim.46), calls=%async_computation.2 | async-start | bytes 262144 | tf_op jit(solution)/shard_map/all_to_all | solution.py:12
  75.7 41.9 %copy-start.2 = (bf16[16,128]{1,0:T(8,128)(2,1)S(1)}, bf16[16,128]{1,0:T(8,128)(2,1)}, u32[]{:S(2)}) copy-start(bf16[16,128]{1,0:T(8,128)(2,1)} %param.15) | copy-start | bytes 12292
  76.5 41.2 %copy-start.1 = (bf16[2048,256]{1,0:T(8,128)(2,1)S(1)}, bf16[2048,256]{1,0:T(8,128)(2,1)}, u32[]{:S(2)}) copy-start(bf16[2048,256]{1,0:T(8,128)(2,1)} %param.17) | copy-start | bytes 3145732
  76.5 16.7 %all-to-all-start.3 = ((f32[16,1,256]{2,1,0:T(1,128)}), f32[16,1,256]{2,1,0:T(1,128)S(1)}, u32[]{:S(2)}, u32[]{:S(2)}) async-start(f32[16,1,256]{2,1,0:T(1,128)} %reshape.117), calls=%async_computation.3 | async-start | bytes 32768 | tf_op jit(solution)/shard_map/all_to_all | solution.py:12
  113.2 16.3 %all-to-all-start.5 = ((f32[16,1,2064]{2,1,0:T(1,128)}), f32[16,1,2064]{2,1,0:T(1,128)S(1)}, u32[]{:S(2)}, u32[]{:S(2)}) async-start(f32[16,1,2064]{2,1,0:T(1,128)} %broadcast_in_dim.50), calls=%async_computation.5 | async-start | bytes 278528 | tf_op jit(solution)/shard_map/all_to_all | solution.py:12
where the time goes:
time: 141 us
  waiting for transfers between devices  43.4 us (31%)
  starting transfers between devices  40 us (28%)
  blocking collectives  38.6 us (27%)
  matrix products  8.61 us (6%)
  other arithmetic  5.06 us (4%)
  local copies, waits for them, and re-layouts  4.91 us (3%)
    all_to_all x4, waiting for transfers between devices, sent_to_all(): return lax.all_to_all(copies, axis, split_axis=0, concat_axis=0, tiled=True)  43.4 us
    all_to_all x4, starting transfers between devices, sent_to_all(): return lax.all_to_all(copies, axis, split_axis=0, concat_axis=0, tiled=True)  40 us
    all_to_all x3, blocking collectives, sent_and_summed(): lax.all_to_all(cut_along(array, dim, length), axis, 0, 0, tiled=True)  38.6 us
    dot_general x1, matrix products, shards(): jnp.einsum('irm,iam->ira', query_vectors, key_cache_rows, preferred_eleme...  3.48 us
    dot_general x1, matrix products, shards(): jnp.einsum('ajq,aqe->aje', softmax_weights.astype(jnp.bfloat16), value_ca...  2.95 us
  transfers between devices with their start and end apart: 4, of which 4 were waited for; matrix products, arithmetic and copies ran while one was open for 2% of the time, Pallas kernels for 0%

commit v1 on v0

v1 whole, which is shorter than its diff:
```python
import functools

import jax
import jax.numpy as jnp
from jax import lax
from jax.experimental import pallas as pl
from jax.experimental.pallas import tpu as pltpu
from jax.sharding import PartitionSpec as P

HD = 128
FLOOR = -1e30
F32 = jnp.float32
BF16 = jnp.bfloat16


def exchanged(blocks, axis):
    return lax.all_to_all(blocks, axis, split_axis=0, concat_axis=0, tiled=True)


def swapped(array, axis):
    return lax.ppermute(array, axis, [(0, 1), (1, 0)])


def call(kernel, shapes, *args, smem=(), mib=16):
    spaces = [pltpu.SMEM if i in smem else pltpu.VMEM for i in range(len(args))]
    return pl.pallas_call(
        kernel,
        out_shape=[jax.ShapeDtypeStruct(s, F32) for s in shapes],
        in_specs=[pl.BlockSpec(memory_space=s) for s in spaces],
        out_specs=[pl.BlockSpec(memory_space=pltpu.VMEM) for _ in shapes],
        compiler_params=pltpu.CompilerParams(vmem_limit_bytes=mib << 20),
    )(*args)


def project(x_ref, g_ref, w_ref, out_ref):
    rows = x_ref.shape[0]
    x = x_ref[...].astype(F32)
    squares = jnp.sum(x * x, axis=1, keepdims=True)
    scaled = x * g_ref[...].astype(F32)
    high = scaled.astype(BF16)
    low = (scaled - high.astype(F32)).astype(BF16)
    both = jnp.concatenate([high, low], axis=0)
    part = jnp.dot(both, w_ref[...], preferred_element_type=F32)
    part = part[:rows] + part[rows:]
    heads = part.shape[1] // HD
    for h in range(heads):
        out_ref[:, h, :] = part[:, h * HD : (h + 1) * HD]
    out_ref[:, heads, :] = jnp.broadcast_to(squares, (rows, HD))


def finish_query(features, got_ref, all_ref, mine_ref):
    n, _, _ = got_ref.shape
    heads = mine_ref.shape[0]
    total = got_ref[0]
    for i in range(1, n):
        total = total + got_ref[i]
    scale = lax.rsqrt(total[heads : heads + 1] / features + 1e-05)
    root = 1.0 / HD**0.5
    mine = (total[:heads] * scale * root).astype(BF16).astype(F32)
    mine_ref[...] = mine
    for i in range(n):
        all_ref[i] = mine


def attend(q_ref, k_ref, v_ref, len_ref, out_ref):
    rows, heads, _ = q_ref.shape
    block = k_ref.shape[1]
    start = lax.axis_index("seq") * block
    at = start + lax.broadcasted_iota(jnp.int32, (heads, block), 1)
    lane = lax.broadcasted_iota(jnp.int32, (heads, HD), 1)
    tops = jnp.zeros((heads, HD), F32)
    totals = jnp.zeros((heads, HD), F32)
    for b in range(rows):
        q = q_ref[b].astype(BF16)
        s = lax.dot_general(q, k_ref[b], (((1,), (1,)), ((), ())), preferred_element_type=F32)
        live = at < len_ref[b]
        top = jnp.max(jnp.where(live, s, FLOOR), axis=1, keepdims=True)
        weights = jnp.where(live, jnp.exp(s - top), 0.0)
        total = jnp.sum(weights, axis=1, keepdims=True)
        out_ref[b, :heads, :] = jnp.dot(
            weights.astype(BF16), v_ref[b], preferred_element_type=F32
        )
        tops = jnp.where(lane == b, top, tops)
        totals = jnp.where(lane == b, total, totals)
    spare = jnp.zeros((HD - 2 * heads, HD), F32)
    turned = jnp.concatenate([tops, totals, spare], axis=0).T
    out_ref[:, heads, :] = turned[:rows]


def combine(got_ref, mine_ref, knew_ref, vnew_ref, all_ref):
    n, _, _ = got_ref.shape
    heads = mine_ref.shape[0]
    me = lax.axis_index("seq")
    chosen = lax.broadcasted_iota(jnp.int32, (knew_ref.shape[0], HD), 0) == me
    k_row = jnp.sum(jnp.where(chosen, knew_ref[...].astype(F32), 0.0), axis=0, keepdims=True)
    v_row = jnp.sum(jnp.where(chosen, vnew_ref[...].astype(F32), 0.0), axis=0, keepdims=True)
    own = jnp.sum(mine_ref[...] * k_row, axis=1, keepdims=True)
    stats = got_ref[:, heads, :]
    stats = jnp.concatenate([stats, jnp.zeros((HD - n, HD), F32)], axis=0).T
    tops = stats[:heads]
    totals = stats[heads : 2 * heads]
    lane = lax.broadcasted_iota(jnp.int32, (heads, HD), 1)
    tops = jnp.where(lane < n, tops, FLOOR)
    top = jnp.maximum(jnp.max(tops, axis=1, keepdims=True), own)
    factor = jnp.exp(tops - top)
    fresh = jnp.exp(own - top)
    total = jnp.sum(factor * totals, axis=1, keepdims=True) + fresh
    summed = fresh * v_row
    for i in range(n):
        summed = summed + factor[:, i : i + 1] * got_ref[i, :heads, :]
    result = (summed / total).astype(BF16).astype(F32)
    for i in range(n):
        all_ref[i] = result


def project_out(a_ref, w_ref, kept_ref, given_ref):
    _, heads, _ = a_ref.shape
    lines = jnp.concatenate([a_ref[:, h, :] for h in range(heads)], axis=1).astype(BF16)
    out = jnp.dot(lines, w_ref[...], preferred_element_type=F32)
    half = out.shape[1] // 2
    first = lax.axis_index("head") == 0
    left, right = out[:, :half], out[:, half:]
    kept_ref[...] = jnp.where(first, left, right)
    given_ref[...] = jnp.where(first, right, left)


def shards(
    hidden_in,
    norm_gain_vector,
    w_query,
    key_cache_rows,
    value_cache_rows,
    k_new,
    v_new,
    lengths,
    w_out,
):
    rows, width = hidden_in.shape
    heads = w_query.shape[1] // HD
    n = lax.axis_size("seq")
    assert rows == n and 2 * heads <= HD
    tall = (n, heads + 8, HD)
    flat = (n, heads, HD)
    (sent,) = call(project, [tall], hidden_in, norm_gain_vector.reshape(1, -1), w_query)
    got = exchanged(sent, "seq")
    sent, mine = call(functools.partial(finish_query, width * n), [flat, flat[1:]], got)
    queries = exchanged(sent, "seq")
    (sent,) = call(
        attend, [tall], queries, key_cache_rows, value_cache_rows, lengths, smem=(3,), mib=24
    )
    got = exchanged(sent, "seq")
    (sent,) = call(combine, [flat], got, mine, k_new, v_new)
    attended = exchanged(sent, "seq")
    half = (rows, w_out.shape[1] // 2)
    kept, given = call(project_out, [half, half], attended, w_out)
    return kept + swapped(given, "head")


def solution(mesh):
    placed = (
        P(("groups", "batch"), "seq"),
        P("seq"),
        P("seq", "head"),
        P(("groups", "batch"), "seq", None),
        P(("groups", "batch"), "seq", None),
        P(("groups", "batch"), None),
        P(("groups", "batch"), None),
        P(("groups", "batch")),
        P("head", "seq"),
    )
    return jax.shard_map(
        shards,
        mesh=mesh,
        in_specs=placed,
        out_specs=P(("groups", "batch"), ("seq", "head")),
        check_vma=False,
    )
```

time: 141 us -> 116 us (0.82)
  blocking collectives: 38.6 us -> 96.4 us
  waiting for transfers between devices: 43.4 us -> 0.83 us
  starting transfers between devices: 40 us -> 3.8 us
  matrix products: 8.61 us -> 0 us
  Pallas kernels: 0 us -> 6.3 us
  other arithmetic: 5.06 us -> 0.6 us
  local copies, waits for them, and re-layouts: 4.91 us -> 7.62 us
    all_to_all x3 -> x4, blocking collectives: 38.6 us -> 96.4 us  [exchanged(): return lax.all_to_all(blocks, axis, split_axis=0, concat_axis=0, tiled=True)]
    all_to_all x4 -> x0, waiting for transfers between devices: 43.4 us -> none  [sent_to_all(): return lax.all_to_all(copies, axis, split_axis=0, concat_axis=0, tiled=True)]
    all_to_all x4 -> x0, starting transfers between devices: 40 us -> none  [sent_to_all(): return lax.all_to_all(copies, axis, split_axis=0, concat_axis=0, tiled=True)]
    dot_general x5 -> x0, matrix products: 8.61 us -> none  [the longest x1 3.48 us: shards(): jnp.einsum('irm,iam->ira', query_vectors, key_cache_rows, preferred_eleme...]
    pallas_call x0 -> x5, Pallas kernels: none -> 6.3 us  [call(): pl.pallas_call(kernel, out_shape=[jax.ShapeDtypeStruct(s, F32) for s in s...]
    unnamed x9 -> x16, local copies, waits for them, and re-layouts: 0.82 us -> 6.96 us
    ppermute x0 -> x1, starting transfers between devices: none -> 3.8 us  [swapped(): return lax.ppermute(array, axis, [(0, 1), (1, 0)])]
    broadcast_in_dim x4 -> x0, local copies, waits for them, and re-layouts: 2.05 us -> none  [sent_to_all(): copies = jnp.broadcast_to(array, (lax.axis_size(axis), *array.shape))]
  transfers between devices with their start and end apart: 4 -> 1, of which waited for: 4 -> 1; matrix products, arithmetic and copies ran while one was open for 2% -> 0% of each run, Pallas kernels for 0% -> 0%
where the time goes in v1:
time: 116 us
  blocking collectives  96.4 us (83%)
  local copies, waits for them, and re-layouts  7.62 us (7%)
  Pallas kernels  6.3 us (5%)
  starting transfers between devices  3.8 us (3%)
    all_to_all x4, blocking collectives, exchanged(): return lax.all_to_all(blocks, axis, split_axis=0, concat_axis=0, tiled=True)  96.4 us
    unnamed x16, local copies, waits for them, and re-layouts  6.96 us
    pallas_call x5, Pallas kernels, call(): pl.pallas_call(kernel, out_shape=[jax.ShapeDtypeStruct(s, F32) for s in s...  6.3 us
    ppermute x1, starting transfers between devices, swapped(): return lax.ppermute(array, axis, [(0, 1), (1, 0)])  3.8 us
  transfers between devices with their start and end apart: 1, of which 1 were waited for; matrix products, arithmetic and copies ran while one was open for 0% of the time, Pallas kernels for 0%

profile of v1, /device:TPU:33, one launch (start us, length us, event | category | flops | bytes accessed | tf_op | source)
XLA Modules:
  0.0 115.6 jit_solution(4539973795366521297)
XLA Ops:
  0.0 0.7 reshape.3.g_ref
  0.7 0.0 copy-start.3
  0.7 1.2 %copy-done.3 = bf16[256,2048]{1,0:T(8,128)(2,1)S(1)} copy-done((bf16[256,2048]{1,0:T(8,128)(2,1)S(1)}, bf16[256,2048]{1,0:T(8,128)(2,1)}, u32[]{:S(2)}) %copy-start.3) | copy-done | bytes 1048600
  1.9 0.0 copy-start.4
  1.9 0.7 copy-done.4
  2.6 0.3 shard_map.91
  2.9 36.6 %all_to_all.20.got_ref = f32[16,24,128]{2,1,0:T(8,128)S(1)} all-to-all(f32[16,24,128]{2,1,0:T(8,128)S(1)} %shard_map.91), channel_id=1, replica_groups=mesh['groups'=2,'seq'=16,'batch'=4,'head'=2] {'seq'}, dimensions={0} | all-to-all | bytes 393216 | tf_op jit(solution)/shard_map/all_to_all | solution.py:17
  39.5 20.7 %all_to_all.21.q_ref = f32[16,16,128]{2,1,0:T(8,128)S(1)} all-to-all(f32[16,16,128]{2,1,0:T(8,128)S(1)} %get-tuple-element.9), channel_id=1, replica_groups=mesh['groups'=2,'seq'=16,'batch'=4,'head'=2] {'seq'}, dimensions={0} | all-to-all | bytes 262144 | tf_op jit(solution)/shard_map/all_to_all | solution.py:17
  60.2 0.0 copy-start
  60.2 2.2 %copy-done = bf16[16,1024,128]{2,1,0:T(8,128)(2,1)S(1)} copy-done((bf16[16,1024,128]{2,1,0:T(8,128)(2,1)S(1)}, bf16[16,1024,128]{2,1,0:T(8,128)(2,1)}, u32[]{:S(2)}) %copy-start) | copy-done | bytes 4194328
  62.4 0.0 copy-start.1
  62.4 2.2 %copy-done.1 = bf16[16,1024,128]{2,1,0:T(8,128)(2,1)S(1)} copy-done((bf16[16,1024,128]{2,1,0:T(8,128)(2,1)S(1)}, bf16[16,1024,128]{2,1,0:T(8,128)(2,1)}, u32[]{:S(2)}) %copy-start.1) | copy-done | bytes 4194328
  64.6 0.0 copy-start.7
  64.6 0.7 copy-done.7
  65.2 0.0 copy-start.5
  65.2 0.0 copy-start.6
  65.2 0.0 copy-start.2
  65.2 5.3 %shard_map.93 = f32[16,24,128]{2,1,0:T(8,128)S(1)} custom-call(f32[16,16,128]{2,1,0:T(8,128)S(1)} %all_to_all.21.q_ref, bf16[16,1024,128]{2,1,0:T(8,128)(2,1)S(1)} %copy-done, bf16[16,1024,128]{2,1,0:T(8,128)(2,1)S(1)} %copy-done.1, s32[16]{0:T(128)S(1)} %copy-done.7), custom_call_target="tpu_custom_call" | custom-call | tf_op jit(solution)/shard_map/pallas_call | solution.py:26
  70.6 18.3 %all_to_all.22.got_ref = f32[16,24,128]{2,1,0:T(8,128)S(1)} all-to-all(f32[16,24,128]{2,1,0:T(8,128)S(1)} %shard_map.93), channel_id=1, replica_groups=mesh['groups'=2,'seq'=16,'batch'=4,'head'=2] {'seq'}, dimensions={0} | all-to-all | bytes 393216 | tf_op jit(solution)/shard_map/all_to_all | solution.py:17
  88.9 0.0 copy-done.5
  88.9 0.0 copy-done.6
  88.9 0.4 shard_map.94
  89.3 20.8 %all_to_all.23.a_ref = f32[16,16,128]{2,1,0:T(8,128)S(1)} all-to-all(f32[16,16,128]{2,1,0:T(8,128)S(1)} %shard_map.94), channel_id=1, replica_groups=mesh['groups'=2,'seq'=16,'batch'=4,'head'=2] {'seq'}, dimensions={0} | all-to-all | bytes 262144 | tf_op jit(solution)/shard_map/all_to_all | solution.py:17
  110.1 0.0 copy-done.2
  110.1 0.3 shard_map.95
  110.3 3.8 %collective-permute-start = (f32[16,128]{1,0:T(8,128)S(1)}, f32[16,128]{1,0:T(8,128)S(1)}, u32[]{:S(2)}, u32[]{:S(2)}) collective-permute-start(f32[16,128]{1,0:T(8,128)S(1)} %get-tuple-element.12), channel_id=1, source_target_pairs={{0,1},{1,0},{2,3},{3,2},{4,5},{5,4},{6,7},{7,6},{8,9},{9,8},{10,11... | collective-permute-start | bytes 24584 | tf_op jit(solution)/shard_map/ppermute | solution.py:21
  114.1 0.8 collective-permute-done
  115.0 0.6 add.3
  (1 shorter events, 0.0 us)
Async XLA Ops:
  0.7 1.2 %copy-start.3 = (bf16[256,2048]{1,0:T(8,128)(2,1)S(1)}, bf16[256,2048]{1,0:T(8,128)(2,1)}, u32[]{:S(2)}) copy-start(bf16[256,2048]{1,0:T(8,128)(2,1)} %w_ref.2) | copy-start | bytes 3145732
  1.9 0.7 copy-start.4
  60.2 2.2 %copy-start = (bf16[16,1024,128]{2,1,0:T(8,128)(2,1)S(1)}, bf16[16,1024,128]{2,1,0:T(8,128)(2,1)}, u32[]{:S(2)}) copy-start(bf16[16,1024,128]{2,1,0:T(8,128)(2,1)} %k_ref.1) | copy-start | bytes 12582916
  62.4 2.2 %copy-start.1 = (bf16[16,1024,128]{2,1,0:T(8,128)(2,1)S(1)}, bf16[16,1024,128]{2,1,0:T(8,128)(2,1)}, u32[]{:S(2)}) copy-start(bf16[16,1024,128]{2,1,0:T(8,128)(2,1)} %v_ref.1) | copy-start | bytes 12582916
  64.6 0.7 copy-start.7
  65.2 23.7 %copy-start.5 = (bf16[16,128]{1,0:T(8,128)(2,1)S(1)}, bf16[16,128]{1,0:T(8,128)(2,1)}, u32[]{:S(2)}) copy-start(bf16[16,128]{1,0:T(8,128)(2,1)} %knew_ref.1) | copy-start | bytes 12292
  65.2 23.7 %copy-start.6 = (bf16[16,128]{1,0:T(8,128)(2,1)S(1)}, bf16[16,128]{1,0:T(8,128)(2,1)}, u32[]{:S(2)}) copy-start(bf16[16,128]{1,0:T(8,128)(2,1)} %vnew_ref.1) | copy-start | bytes 12292
  65.2 44.8 %copy-start.2 = (bf16[2048,256]{1,0:T(8,128)(2,1)S(1)}, bf16[2048,256]{1,0:T(8,128)(2,1)}, u32[]{:S(2)}) copy-start(bf16[2048,256]{1,0:T(8,128)(2,1)} %w_ref.3) | copy-start | bytes 3145732
  110.3 4.6 %collective-permute-start = (f32[16,128]{1,0:T(8,128)S(1)}, f32[16,128]{1,0:T(8,128)S(1)}, u32[]{:S(2)}, u32[]{:S(2)}) collective-permute-start(f32[16,128]{1,0:T(8,128)S(1)} %get-tuple-element.12), channel_id=1, source_target_pairs={{0,1},{1,0},{2,3},{3,2},{4,5},{5,4},{6,7},{7,6},{8,9},{9,8},{10,11... | collective-permute-start | bytes 24584 | tf_op jit(solution)/shard_map/ppermute | solution.py:21

commit v2 on v1

--- a/solution.py
+++ b/solution.py
@@ -17,44 +17,64 @@
     return lax.all_to_all(blocks, axis, split_axis=0, concat_axis=0, tiled=True)
 
 
+def parts_exchanged(lines):
+    return exchanged(lines.reshape(-1, 1, HD), "seq").reshape(lines.shape)
+
+
 def swapped(array, axis):
     return lax.ppermute(array, axis, [(0, 1), (1, 0)])
 
 
-def call(kernel, shapes, *args, smem=(), mib=16):
-    spaces = [pltpu.SMEM if i in smem else pltpu.VMEM for i in range(len(args))]
+def call(kernel, shapes, *args, away=(), scratch=(), mib=16):
+    spaces = [pltpu.HBM if i in away else pltpu.VMEM for i in range(len(args))]
+    args = [
+        pltpu.with_memory_space_constraint(a, pltpu.HBM) if i in away else a
+        for i, a in enumerate(args)
+    ]
     return pl.pallas_call(
         kernel,
         out_shape=[jax.ShapeDtypeStruct(s, F32) for s in shapes],
         in_specs=[pl.BlockSpec(memory_space=s) for s in spaces],
         out_specs=[pl.BlockSpec(memory_space=pltpu.VMEM) for _ in shapes],
+        scratch_shapes=scratch,
         compiler_params=pltpu.CompilerParams(vmem_limit_bytes=mib << 20),
     )(*args)
 
 
-def project(x_ref, g_ref, w_ref, out_ref):
-    rows = x_ref.shape[0]
+def project(x_hbm, g_hbm, w_hbm, out_ref, x_ref, g_ref, w_ref, sems):
+    pairs = ((x_hbm, x_ref), (g_hbm, g_ref), (w_hbm, w_ref))
+    copies = [pltpu.make_async_copy(a, b, sems.at[i]) for i, (a, b) in enumerate(pairs)]
+    for copy in copies:
+        copy.start()
+    copies[0].wait()
+    copies[1].wait()
+    rows, width = x_ref.shape
     x = x_ref[...].astype(F32)
     squares = jnp.sum(x * x, axis=1, keepdims=True)
-    scaled = x * g_ref[...].astype(F32)
+    scaled = x * g_ref[...].astype(F32).reshape(1, width)
     high = scaled.astype(BF16)
     low = (scaled - high.astype(F32)).astype(BF16)
     both = jnp.concatenate([high, low], axis=0)
+    copies[2].wait()
     part = jnp.dot(both, w_ref[...], preferred_element_type=F32)
     part = part[:rows] + part[rows:]
     heads = part.shape[1] // HD
-    for h in range(heads):
-        out_ref[:, h, :] = part[:, h * HD : (h + 1) * HD]
-    out_ref[:, heads, :] = jnp.broadcast_to(squares, (rows, HD))
+    squares = jnp.broadcast_to(squares, (rows, HD))
+    for b in range(rows):
+        lines = [part[b : b + 1, h * HD : (h + 1) * HD] for h in range(heads)]
+        out_ref[b * (heads + 1) : (b + 1) * (heads + 1), :] = jnp.concatenate(
+            [*lines, squares[b : b + 1]], axis=0
+        )
 
 
 def finish_query(features, got_ref, all_ref, mine_ref):
-    n, _, _ = got_ref.shape
     heads = mine_ref.shape[0]
-    total = got_ref[0]
+    tall = heads + 1
+    n = got_ref.shape[0] // tall
+    total = got_ref[:tall, :]
     for i in range(1, n):
-        total = total + got_ref[i]
-    scale = lax.rsqrt(total[heads : heads + 1] / features + 1e-05)
+        total = total + got_ref[i * tall : (i + 1) * tall, :]
+    scale = lax.rsqrt(total[heads:tall] / features + 1e-05)
     root = 1.0 / HD**0.5
     mine = (total[:heads] * scale * root).astype(BF16).astype(F32)
     mine_ref[...] = mine
@@ -62,41 +82,61 @@
         all_ref[i] = mine
 
 
-def attend(q_ref, k_ref, v_ref, len_ref, out_ref):
+def attend(q_ref, k_hbm, v_hbm, len_hbm, out_ref, k_ref, v_ref, len_ref, sems, len_sem):
     rows, heads, _ = q_ref.shape
     block = k_ref.shape[1]
+    chunks = sems.shape[1]
+    step = rows // chunks
+    used = pltpu.make_async_copy(len_hbm, len_ref, len_sem)
+    used.start()
+    copies = []
+    for c in range(chunks):
+        at = pl.ds(c * step, step)
+        keys = pltpu.make_async_copy(k_hbm.at[at], k_ref.at[at], sems.at[0, c])
+        values = pltpu.make_async_copy(v_hbm.at[at], v_ref.at[at], sems.at[1, c])
+        keys.start()
+        values.start()
+        copies.append((keys, values))
+    used.wait()
     start = lax.axis_index("seq") * block
     at = start + lax.broadcasted_iota(jnp.int32, (heads, block), 1)
     lane = lax.broadcasted_iota(jnp.int32, (heads, HD), 1)
     tops = jnp.zeros((heads, HD), F32)
     totals = jnp.zeros((heads, HD), F32)
+    tall = heads + 1
     for b in range(rows):
+        if b % step == 0:
+            copies[b // step][0].wait()
         q = q_ref[b].astype(BF16)
         s = lax.dot_general(q, k_ref[b], (((1,), (1,)), ((), ())), preferred_element_type=F32)
         live = at < len_ref[b]
         top = jnp.max(jnp.where(live, s, FLOOR), axis=1, keepdims=True)
         weights = jnp.where(live, jnp.exp(s - top), 0.0)
         total = jnp.sum(weights, axis=1, keepdims=True)
-        out_ref[b, :heads, :] = jnp.dot(
+        if b % step == 0:
+            copies[b // step][1].wait()
+        out_ref[b * tall : b * tall + heads, :] = jnp.dot(
             weights.astype(BF16), v_ref[b], preferred_element_type=F32
         )
         tops = jnp.where(lane == b, top, tops)
         totals = jnp.where(lane == b, total, totals)
     spare = jnp.zeros((HD - 2 * heads, HD), F32)
     turned = jnp.concatenate([tops, totals, spare], axis=0).T
-    out_ref[:, heads, :] = turned[:rows]
+    for b in range(rows):
+        out_ref[b * tall + heads : (b + 1) * tall, :] = turned[b : b + 1]
 
 
 def combine(got_ref, mine_ref, knew_ref, vnew_ref, all_ref):
-    n, _, _ = got_ref.shape
     heads = mine_ref.shape[0]
+    tall = heads + 1
+    n = got_ref.shape[0] // tall
     me = lax.axis_index("seq")
     chosen = lax.broadcasted_iota(jnp.int32, (knew_ref.shape[0], HD), 0) == me
     k_row = jnp.sum(jnp.where(chosen, knew_ref[...].astype(F32), 0.0), axis=0, keepdims=True)
     v_row = jnp.sum(jnp.where(chosen, vnew_ref[...].astype(F32), 0.0), axis=0, keepdims=True)
     own = jnp.sum(mine_ref[...] * k_row, axis=1, keepdims=True)
-    stats = got_ref[:, heads, :]
-    stats = jnp.concatenate([stats, jnp.zeros((HD - n, HD), F32)], axis=0).T
+    stats = [got_ref[i * tall + heads : (i + 1) * tall, :] for i in range(n)]
+    stats = jnp.concatenate([*stats, jnp.zeros((HD - n, HD), F32)], axis=0).T
     tops = stats[:heads]
     totals = stats[heads : 2 * heads]
     lane = lax.broadcasted_iota(jnp.int32, (heads, HD), 1)
@@ -107,7 +147,7 @@
     total = jnp.sum(factor * totals, axis=1, keepdims=True) + fresh
     summed = fresh * v_row
     for i in range(n):
-        summed = summed + factor[:, i : i + 1] * got_ref[i, :heads, :]
+        summed = summed + factor[:, i : i + 1] * got_ref[i * tall : i * tall + heads, :]
     result = (summed / total).astype(BF16).astype(F32)
     for i in range(n):
         all_ref[i] = result
@@ -139,16 +179,44 @@
     heads = w_query.shape[1] // HD
     n = lax.axis_size("seq")
     assert rows == n and 2 * heads <= HD
-    tall = (n, heads + 8, HD)
+    tall = (n * (heads + 1), HD)
     flat = (n, heads, HD)
-    (sent,) = call(project, [tall], hidden_in, norm_gain_vector.reshape(1, -1), w_query)
-    got = exchanged(sent, "seq")
+    dma = pltpu.SemaphoreType.DMA
+    (sent,) = call(
+        project,
+        [tall],
+        hidden_in,
+        norm_gain_vector,
+        w_query,
+        away=(0, 1, 2),
+        scratch=[
+            pltpu.VMEM(hidden_in.shape, BF16),
+            pltpu.VMEM(norm_gain_vector.shape, BF16),
+            pltpu.VMEM(w_query.shape, BF16),
+            dma((3,)),
+        ],
+    )
+    got = parts_exchanged(sent)
     sent, mine = call(functools.partial(finish_query, width * n), [flat, flat[1:]], got)
     queries = exchanged(sent, "seq")
     (sent,) = call(
-        attend, [tall], queries, key_cache_rows, value_cache_rows, lengths, smem=(3,), mib=24
-    )
-    got = exchanged(sent, "seq")
+        attend,
+        [tall],
+        queries,
+        key_cache_rows,
+        value_cache_rows,
+        lengths,
+        away=(1, 2, 3),
+        scratch=[
+            pltpu.VMEM(key_cache_rows.shape, BF16),
+            pltpu.VMEM(value_cache_rows.shape, BF16),
+            pltpu.SMEM(lengths.shape, jnp.int32),
+            dma((2, rows // 2)),
+            dma(()),
+        ],
+        mib=24,
+    )
+    got = parts_exchanged(sent)
     (sent,) = call(combine, [flat], got, mine, k_new, v_new)
     attended = exchanged(sent, "seq")
     half = (rows, w_out.shape[1] // 2)

time: 116 us -> 105 us (0.905)
  local copies, waits for them, and re-layouts: 7.62 us -> 0.01 us
  blocking collectives: 96.4 us -> 89.3 us
  Pallas kernels: 6.3 us -> 9.97 us
    all_to_all x4, blocking collectives: 96.4 us -> 89.3 us  [exchanged(): return lax.all_to_all(blocks, axis, split_axis=0, concat_axis=0, tiled=True)]
    unnamed x16 -> x6, local copies, waits for them, and re-layouts: 6.96 us -> 0.01 us
    pallas_call x5, Pallas kernels: 6.3 us -> 9.97 us  [call(): pl.pallas_call(kernel, out_shape=[jax.ShapeDtypeStruct(s, F32) for s in s...]
where the time goes in v2:
time: 105 us
  blocking collectives  89.3 us (85%)
  Pallas kernels  9.97 us (9%)
  starting transfers between devices  4.19 us (4%)
    all_to_all x4, blocking collectives, exchanged(): return lax.all_to_all(blocks, axis, split_axis=0, concat_axis=0, tiled=True)  89.3 us
    pallas_call x5, Pallas kernels, call(): pl.pallas_call(kernel, out_shape=[jax.ShapeDtypeStruct(s, F32) for s in s...  9.97 us
    ppermute x1, starting transfers between devices, swapped(): return lax.ppermute(array, axis, [(0, 1), (1, 0)])  4.19 us
  transfers between devices with their start and end apart: 1, of which 1 were waited for; matrix products, arithmetic and copies ran while one was open for 0% of the time, Pallas kernels for 0%

profile of v2, /device:TPU:33, one launch (start us, length us, event | category | flops | bytes accessed | tf_op | source)
XLA Modules:
  0.0 105.0 jit_solution(5251201358492987984)
XLA Ops:
  0.0 1.6 %shard_map.91 = f32[272,128]{1,0:T(8,128)S(1)} custom-call(bf16[16,256]{1,0:T(8,128)(2,1)} %x_hbm.1, bf16[256]{0:T(256)(128)(2,1)} %g_hbm.1, bf16[256,2048]{1,0:T(8,128)(2,1)} %w_hbm.1), custom_call_target="tpu_custom_call" | custom-call | tf_op jit(solution)/shard_map/pallas_call | solution.py:34
  1.6 36.1 %all_to_all.20 = f32[272,1,128]{2,1,0:T(1,128)S(1)} all-to-all(f32[272,1,128]{2,1,0:T(1,128)S(1)} %bitcast.9), channel_id=1, replica_groups=mesh['groups'=2,'seq'=16,'batch'=4,'head'=2] {'seq'}, dimensions={0} | all-to-all | bytes 278528 | tf_op jit(solution)/shard_map/all_to_all | solution.py:17
  37.8 18.4 %all_to_all.21.q_ref = f32[16,16,128]{2,1,0:T(8,128)S(1)} all-to-all(f32[16,16,128]{2,1,0:T(8,128)S(1)} %get-tuple-element.9), channel_id=1, replica_groups=mesh['groups'=2,'seq'=16,'batch'=4,'head'=2] {'seq'}, dimensions={0} | all-to-all | bytes 262144 | tf_op jit(solution)/shard_map/all_to_all | solution.py:17
  56.1 0.0 copy-start.1
  56.1 0.0 copy-start.2
  56.1 0.0 copy-start
  56.1 7.7 %shard_map.93 = f32[272,128]{1,0:T(8,128)S(1)} custom-call(f32[16,16,128]{2,1,0:T(8,128)S(1)} %all_to_all.21.q_ref, bf16[16,1024,128]{2,1,0:T(8,128)(2,1)} %k_hbm.1, bf16[16,1024,128]{2,1,0:T(8,128)(2,1)} %v_hbm.1, s32[16]{0:T(128)} %len_hbm.1), custom_call_target="tpu_custom_call" | custom-call | tf_op jit(solution)/shard_map/pallas_call | solution.py:34
  63.9 17.4 %all_to_all.22 = f32[272,1,128]{2,1,0:T(1,128)S(1)} all-to-all(f32[272,1,128]{2,1,0:T(1,128)S(1)} %bitcast.8), channel_id=1, replica_groups=mesh['groups'=2,'seq'=16,'batch'=4,'head'=2] {'seq'}, dimensions={0} | all-to-all | bytes 278528 | tf_op jit(solution)/shard_map/all_to_all | solution.py:17
  81.3 0.0 copy-done.1
  81.3 0.0 copy-done.2
  81.3 0.4 shard_map.94
  81.7 17.4 %all_to_all.23.a_ref = f32[16,16,128]{2,1,0:T(8,128)S(1)} all-to-all(f32[16,16,128]{2,1,0:T(8,128)S(1)} %shard_map.94), channel_id=1, replica_groups=mesh['groups'=2,'seq'=16,'batch'=4,'head'=2] {'seq'}, dimensions={0} | all-to-all | bytes 262144 | tf_op jit(solution)/shard_map/all_to_all | solution.py:17
  99.1 0.0 copy-done
  99.1 0.3 shard_map.95
  99.3 4.2 %collective-permute-start = (f32[16,128]{1,0:T(8,128)S(1)}, f32[16,128]{1,0:T(8,128)S(1)}, u32[]{:S(2)}, u32[]{:S(2)}) collective-permute-start(f32[16,128]{1,0:T(8,128)S(1)} %get-tuple-element.12), channel_id=1, source_target_pairs={{0,1},{1,0},{2,3},{3,2},{4,5},{5,4},{6,7},{7,6},{8,9},{9,8},{10,11... | collective-permute-start | bytes 24584 | tf_op jit(solution)/shard_map/ppermute | solution.py:25
  103.5 0.8 collective-permute-done
  104.4 0.6 add.3
  (1 shorter events, 0.0 us)
Async XLA Ops:
  56.1 25.2 %copy-start.1 = (bf16[16,128]{1,0:T(8,128)(2,1)S(1)}, bf16[16,128]{1,0:T(8,128)(2,1)}, u32[]{:S(2)}) copy-start(bf16[16,128]{1,0:T(8,128)(2,1)} %knew_ref.1) | copy-start | bytes 12292
  56.1 25.2 %copy-start.2 = (bf16[16,128]{1,0:T(8,128)(2,1)S(1)}, bf16[16,128]{1,0:T(8,128)(2,1)}, u32[]{:S(2)}) copy-start(bf16[16,128]{1,0:T(8,128)(2,1)} %vnew_ref.1) | copy-start | bytes 12292
  56.1 42.9 %copy-start = (bf16[2048,256]{1,0:T(8,128)(2,1)S(1)}, bf16[2048,256]{1,0:T(8,128)(2,1)}, u32[]{:S(2)}) copy-start(bf16[2048,256]{1,0:T(8,128)(2,1)} %w_ref.1) | copy-start | bytes 3145732
  99.3 5.0 %collective-permute-start = (f32[16,128]{1,0:T(8,128)S(1)}, f32[16,128]{1,0:T(8,128)S(1)}, u32[]{:S(2)}, u32[]{:S(2)}) collective-permute-start(f32[16,128]{1,0:T(8,128)S(1)} %get-tuple-element.12), channel_id=1, source_target_pairs={{0,1},{1,0},{2,3},{3,2},{4,5},{5,4},{6,7},{7,6},{8,9},{9,8},{10,11... | collective-permute-start | bytes 24584 | tf_op jit(solution)/shard_map/ppermute | solution.py:25
